TPU v7x, 32 devices: a whole 2x2x4 slice. The times are simulated.
32 devices in a mesh: rows: 8 (over z, x), cols: 4 (over y, core).
Axes of the slice: x: 2, y: 2, z: 4, core: 2. Of those that a mesh axis runs over, the one named last changes fastest.
Arguments:
- basis: float32 [8192, 4096], P('rows', 'cols'), may hold values from -119.66257 to 119.66257, as said below
- block: float32 [8192, 512], P('rows', 'cols'), may hold values from -1800 to 1800
Outputs:
- ortho: float32 [8192, 512], P('rows', 'cols')
- factors: float32 [4, 128, 128], P('cols')
Inputs may be any that keep to these rules, and one draw needn't show every extreme that they name: Under the inner product (sum over rows divided by 8192) the basis columns have squared norms between 0.6 and 1.9, and inner products of distinct basis columns are at most 0.05 in magnitude.
All inputs are finite; a program needn't handle non-finite values.
Results may differ from a plain program's by a relative error of at most 0.000076.
Values sent between devices are 32-bit elements; how exact they have to be, the bound alone decides.
A program may use at most 64 MiB of HBM per device.

v0:
```python
import jax
import jax.numpy as jnp
from jax import lax
from jax.sharding import PartitionSpec as P

BLK = 128


def solve_block(lower_factor, vectors):
    return jax.scipy.linalg.solve_triangular(lower_factor, vectors, lower=True)


def body(basis, block):
    highest = lax.Precision.HIGHEST
    local_rows = basis.shape[0]
    inverse = 1.0 / (local_rows * lax.axis_size("rows"))
    width = block.shape[1]
    column_index = lax.axis_index("cols")

    def project(piece):
        return (
            lax.dot_general(
                basis,
                piece,
                (((0,), (0,)), ((), ())),
                precision=highest,
                preferred_element_type=jnp.float32,
            )
            * inverse
        )

    def expand(coef):
        return jnp.dot(basis, coef, precision=highest, preferred_element_type=jnp.float32)

    terms_one = project(lax.all_gather(block, "cols", axis=1, tiled=True))
    coef_one = lax.psum(terms_one, "rows")
    placed = lax.dynamic_update_slice_in_dim(
        jnp.zeros((local_rows, coef_one.shape[1]), jnp.float32), block, column_index * width, 1
    )
    first_whole = lax.psum(placed - expand(coef_one), "cols")
    terms_two = project(first_whole)
    first = lax.dynamic_slice_in_dim(first_whole, column_index * width, width, 1)
    coef_two = lax.psum(terms_two, "rows")
    second = first - lax.psum_scatter(expand(coef_two), "cols", scatter_dimension=1, tiled=True)
    blocks = width // BLK
    pieces = second.reshape(local_rows, blocks, BLK)
    gram = jnp.einsum("mbi,mbj->bij", pieces, pieces, precision=highest) * inverse
    gram = lax.psum(gram, "rows")
    lower_factor = jnp.linalg.cholesky(gram)
    solved = jax.vmap(solve_block)(lower_factor, jnp.transpose(pieces, (1, 2, 0)))
    ortho = jnp.transpose(solved, (2, 0, 1)).reshape(local_rows, width)
    return (ortho, jnp.transpose(lower_factor, (0, 2, 1)))


def solution(mesh):
    placed = (P("rows", "cols"), P("rows", "cols"))
    return jax.shard_map(
        body,
        mesh=mesh,
        in_specs=placed,
        out_specs=(P("rows", "cols"), P("cols", None, None)),
        check_vma=False,
    )
```

profile of v0, /device:TPU:0, one launch (start us, length us, event | category | flops | bytes accessed | tf_op | source)
XLA Modules:
  0.0 476.0 jit_solution(7517272405939530119)
XLA Ops:
  7.2 0.0 all-gather.2.cloned.1.call-start
  7.2 0.7 all-gather.2.cloned.1.call-update
  7.9 0.0 all-reduce.5.cloned.1.call-start
  7.9 27.2 %all-gather.2.cloned.1.call-done = f32[1024,512]{1,0:T(8,128)} async-done(((f32[1024,128]{1,0:T(8,128)}), f32[1024,512]{1,0:T(8,128)}) %all-gather.2.cloned.1.call-update) | async-done | bytes 2097168 | tf_op jit(solution)/shard_map/all_gather | solution.py:35
  35.1 10.2 %convolution_multiply_fusion = f32[1024,512]{1,0:T(8,128)} fusion(f32[1024,1024]{1,0:T(8,128)} %param.2, f32[1024,512]{1,0:T(8,128)} %all-gather.2.cloned.1.call-done), kind=kOutput, calls=%fused_computation.3 | convolution fusion | flops 6442975232 | bytes 8388608 | tf_op jit(solution)/shard_map/dot_general | solution.py:22
  45.3 0.0 all-reduce.7.cloned.1.call-start
  45.4 1.0 copy-done.1
  46.3 0.2 copy.4
  46.5 0.2 broadcast_in_dim.7
  46.8 0.1 constant_dynamic-update-slice_fusion
  46.8 100.9 %all-reduce.5.cloned.1.call-done = f32[1024,512]{1,0:T(8,128)} async-done(((f32[1024,512]{1,0:T(8,128)}), f32[1024,512]{1,0:T(8,128)}) %all-reduce.5.cloned.1.call-update) | async-done | bytes 2097168 | tf_op jit(solution)/shard_map/psum | solution.py:36
  147.8 16.7 %bitcast_subtract_fusion = f32[1024,512]{0,1:T(8,128)} fusion(f32[1024,512]{0,1:T(8,128)S(1)} %constant_dynamic-update-slice_fusion, f32[1024,512]{1,0:T(8,128)} %all-reduce.5.cloned.1.call-done, f32[1024,1024]{1,0:T(8,128)} %param.2), kind=kOutput, calls=%fused_computation | convolution fusion | flops 6442975232 | bytes 10485760 | tf_op jit(solution)/shard_map/dot_general | solution.py:33
  164.5 0.2 all-reduce.9.cloned.1.call-start
  164.7 50.6 %all-reduce.7.cloned.1.call-done = f32[1024,512]{0,1:T(8,128)} async-done(((f32[1024,512]{0,1:T(8,128)}), f32[1024,512]{0,1:T(8,128)}) %all-reduce.7.cloned.1.call-update) | async-done | bytes 2097168 | tf_op jit(solution)/shard_map/psum | solution.py:40
  215.3 10.2 %multiply_bitcast_fusion = f32[1024,512]{0,1:T(8,128)} fusion(f32[1024,512]{0,1:T(8,128)} %all-reduce.7.cloned.1.call-done, f32[1024,1024]{1,0:T(8,128)} %param.2), kind=kOutput, calls=%fused_computation.1 | convolution fusion | flops 6442975232 | bytes 8388608 | tf_op jit(solution)/shard_map/dot_general | solution.py:22
  225.6 0.0 all-reduce.9.cloned.1.call-update
  225.6 0.0 reduce-scatter.2.cloned.1.call-start
  225.6 102.5 %all-reduce.9.cloned.1.call-done = f32[1024,512]{0,1:T(8,128)} async-done(((f32[1024,512]{0,1:T(8,128)}), f32[1024,512]{0,1:T(8,128)}) %all-reduce.9.cloned.1.call-update) | async-done | bytes 2097168 | tf_op jit(solution)/shard_map/psum | solution.py:43
  328.1 10.3 %convolution_bitcast_fusion = f32[1024,512]{0,1:T(8,128)} fusion(f32[1024,512]{0,1:T(8,128)} %all-reduce.9.cloned.1.call-done, f32[1024,1024]{1,0:T(8,128)} %param.2), kind=kOutput, calls=%fused_computation.2 | convolution fusion | flops 6442450944 | bytes 8388608 | tf_op jit(solution)/shard_map/dot_general | solution.py:33
  338.4 0.3 all-reduce.11.cloned.1.call-start
  338.7 30.3 %reduce-scatter.2.cloned.1.call-done = f32[1024,128]{0,1:T(8,128)} async-done(((f32[1024,512]{0,1:T(8,128)}), f32[1024,128]{0,1:T(8,128)}) %reduce-scatter.2.cloned.1.call-update) | async-done | bytes 524304 | tf_op jit(solution)/shard_map/reduce_scatter | solution.py:44
  369.0 2.5 fusion
  371.5 70.6 %all-reduce.11.cloned.1.call-done = f32[1,128,128]{1,2,0:T(8,128)} async-done(((f32[1,128,128]{1,2,0:T(8,128)}), f32[1,128,128]{1,2,0:T(8,128)}) %all-reduce.11.cloned.1.call-update) | async-done | bytes 65552 | tf_op jit(solution)/shard_map/psum | solution.py:48
  442.2 0.9 copy.6
  443.1 0.9 fusion.3
  444.0 11.7 %custom-call.8 = f32[1,128,128]{2,1,0:T(8,128)S(1)} custom-call(f32[1,128,128]{2,1,0:T(8,128)S(1)} %fusion.3), custom_call_target="Cholesky" | custom-call | tf_op jit(solution)/shard_map/jit(cholesky)/cholesky | solution.py:49
  455.7 0.6 compare_reduce_fusion
  456.4 0.7 fusion.4
  457.0 9.8 %custom-call.9 = f32[1,1,128,128]{2,3,1,0:T(8,128)S(1)} custom-call(f32[1,1,128,128]{3,2,1,0:T(8,128)S(1)} %get-tuple-element.5), custom_call_target="InvertDiagBlocksLowerTriangular" | custom-call | tf_op jit(solution)/shard_map/vmap(jit(_solve_triangular))/triangular_solve | solution.py:10
  466.8 0.6 convolution_bitcast_fusion.1
  467.5 1.0 copy.7
  468.5 0.7 copy.8
  (10 shorter events, 0.1 us)
Async XLA Ops:
  7.2 27.9 %all-gather.2.cloned.1.call-start = ((), (), s32[]{:S(2)}) async-start(), calls=%async_computation.1 | async-start | bytes 2621440 | tf_op jit(solution)/shard_map/all_gather | solution.py:35
  7.9 139.9 %all-reduce.5.cloned.1.call-start = ((), (), s32[]{:S(2)}) async-start(), calls=%async_computation.2 | async-start | bytes 4194304 | tf_op jit(solution)/shard_map/psum | solution.py:36
  45.3 1.0 copy-start.1
  45.3 170.0 %all-reduce.7.cloned.1.call-start = ((), (), s32[]{:S(2)}) async-start(), calls=%async_computation.3 | async-start | bytes 4194304 | tf_op jit(solution)/shard_map/psum | solution.py:40
  164.5 163.6 %all-reduce.9.cloned.1.call-start = ((), (), s32[]{:S(2)}) async-start(), calls=%async_computation.4 | async-start | bytes 4194304 | tf_op jit(solution)/shard_map/psum | solution.py:43
  225.6 143.4 %reduce-scatter.2.cloned.1.call-start = ((), (), s32[]{:S(2)}) async-start(), calls=%async_computation.5 | async-start | bytes 2621440 | tf_op jit(solution)/shard_map/reduce_scatter | solution.py:44
  338.4 30.6 %copy-start = (f32[1024,512]{0,1:T(8,128)S(1)}, f32[1024,512]{0,1:T(8,128)}, u32[]{:S(2)}) copy-start(f32[1024,512]{0,1:T(8,128)} %all-reduce.7.cloned.1.call-done) | copy-start | bytes 6291460
  338.4 103.8 %all-reduce.11.cloned.1.call-start = ((), (), s32[]{:S(2)}) async-start(), calls=%async_computation.6 | async-start | bytes 131072 | tf_op jit(solution)/shard_map/psum | solution.py:48
  369.0 97.8 %copy-start.2 = (f32[1024,128]{0,1:T(8,128)S(1)}, f32[1024,128]{0,1:T(8,128)}, u32[]{:S(2)}) copy-start(f32[1024,128]{0,1:T(8,128)} %reduce-scatter.2.cloned.1.call-done) | copy-start | bytes 1572868
Sparse Core Ops, SparseCore 0:
  9.5 25.5 all-gather.1
  45.4 102.3 all-reduce.4
  164.6 50.6 all-reduce.6
  225.7 102.3 all-reduce.8
  338.5 30.4 reduce-scatter.1
  372.9 69.2 all-reduce.10
where the time goes:
time: 476 us
  waiting for transfers between devices  383 us (80%)
  matrix products  50.5 us (11%)
  other arithmetic  23.7 us (5%)
  between operations  14.2 us (3%)
    psum x1, waiting for transfers between devices, body(): coef_two = lax.psum(terms_two, 'rows')  102 us
    psum x1, waiting for transfers between devices, body(): coef_one = lax.psum(terms_one, 'rows')  101 us
    psum x1, waiting for transfers between devices, body(): gram = lax.psum(gram, 'rows')  70.6 us
    psum x1, waiting for transfers between devices, body(): first_whole = lax.psum(placed - expand(coef_one), 'cols')  50.6 us
    reduce_scatter x1, waiting for transfers between devices, body(): lax.psum_scatter(expand(coef_two), 'cols', scatter_dimension=1, tiled=True)  30.3 us
    all_gather x1, waiting for transfers between devices, body(): terms_one = project(lax.all_gather(block, 'cols', axis=1, tiled=True))  27.2 us
    dot_general x2, matrix products, expand(): jnp.dot(basis, coef, precision=highest, preferred_element_type=jnp.float32)  27 us
    dot_general x2, matrix products, project(): lax.dot_general(basis, piece, (((0,), (0,)), ((), ())), precision=highest...  20.4 us
  transfers between devices with their start and end apart: 6, of which 6 were waited for; matrix products, arithmetic and copies ran while one was open for 0% of the time, Pallas kernels for 0%

commit v1 on v0

v1 whole, which is shorter than its diff:
```python
import functools

import jax
import jax.numpy as jnp
from jax import lax
from jax.experimental import pallas as pl
from jax.experimental.pallas import tpu as pltpu
from jax.sharding import PartitionSpec as P

BLK = 128
PIECES = 4
MESH = pl.DeviceIdType.MESH
F32 = jnp.float32


def greet(axis, others):
    barrier = pltpu.get_barrier_semaphore()
    for other in others:
        pl.semaphore_signal(barrier, inc=1, device_id={axis: other}, device_id_type=MESH)
    pl.semaphore_wait(barrier, len(others))


def send(axis, device, source, target, send_sem, recv_sem):
    return pltpu.make_async_remote_copy(
        src_ref=source,
        dst_ref=target,
        send_sem=send_sem,
        recv_sem=recv_sem,
        device_id={axis: device},
        device_id_type=MESH,
    )


def partners():
    me = lax.axis_index("cols")
    core, side = lax.rem(me, 2), lax.div(me, 2)
    return me, core, side, side * 2 + 1 - core, (1 - side) * 2 + core


def columns(index, width):
    return pl.ds(pl.multiple_of(index * width, width), width)


def gather_kernel(block, out, send_sem, recv_sem):
    me, core, side, mate, across = partners()
    greet("cols", (mate, across))
    rows, width = block.shape
    step = rows // PIECES
    far, near, passed = [], [], []
    for q in range(PIECES):
        part = pl.ds(q * step, step)
        far.append(send("cols", across, block.at[part], out.at[part, columns(me, width)], send_sem.at[0, q], recv_sem.at[0, q]))
        far[-1].start()
    for q in range(PIECES):
        part = pl.ds(q * step, step)
        near.append(send("cols", mate, block.at[part], out.at[part, columns(me, width)], send_sem.at[1, q], recv_sem.at[1, q]))
        near[-1].start()
    out[:, columns(me, width)] = block[...]
    for q in range(PIECES):
        part = pl.ds(q * step, step)
        far[q].wait_recv()
        held = out.at[part, columns(across, width)]
        passed.append(send("cols", mate, held, held, send_sem.at[2, q], recv_sem.at[2, q]))
        passed[-1].start()
    for q in range(PIECES):
        near[q].wait_recv()
        passed[q].wait_recv()
    for copy in far + near + passed:
        copy.wait_send()


def first_kernel(partial, base, out, near_in, chip, far_in, send_sem, recv_sem):
    me, core, side, mate, across = partners()
    greet("cols", (mate, across))
    half = partial.shape[0] // 2
    step = half // PIECES

    def mine(q):
        return pl.ds(pl.multiple_of(core * half + q * step, step), step)

    def others(q):
        return pl.ds(pl.multiple_of((1 - core) * half + q * step, step), step)

    near, far, back = [], [], []
    for q in range(PIECES):
        near.append(send("cols", mate, partial.at[others(q)], near_in.at[q], send_sem.at[0, q], recv_sem.at[0, q]))
        near[-1].start()
    for q in range(PIECES):
        near[q].wait_recv()
        chip[q] = partial[mine(q)] + near_in[q]
        far.append(send("cols", across, chip.at[q], far_in.at[q], send_sem.at[1, q], recv_sem.at[1, q]))
        far[-1].start()
    for q in range(PIECES):
        far[q].wait_recv()
        out[mine(q)] = base[mine(q)] - (chip[q] + far_in[q])
        held = out.at[mine(q)]
        back.append(send("cols", mate, held, held, send_sem.at[2, q], recv_sem.at[2, q]))
        back[-1].start()
    for q in range(PIECES):
        back[q].wait_recv()
    for copy in near + far + back:
        copy.wait_send()


def second_kernel(partial, first, out, near_in, chip, far_in, send_sem, recv_sem):
    me, core, side, mate, across = partners()
    greet("cols", (mate, across))
    rows, width = out.shape
    step = rows // PIECES
    near, far = {}, []
    for kind, there in enumerate((1 - side, side)):
        for q in range(PIECES):
            part = pl.ds(q * step, step)
            source = partial.at[part, columns(there * 2 + 1 - core, width)]
            near[kind, q] = send("cols", mate, source, near_in.at[kind, part], send_sem.at[kind, q], recv_sem.at[kind, q])
            near[kind, q].start()
    for q in range(PIECES):
        part = pl.ds(q * step, step)
        near[0, q].wait_recv()
        chip[part] = partial[part, columns(across, width)] + near_in[0, part]
        far.append(send("cols", across, chip.at[part], far_in.at[part], send_sem.at[2, q], recv_sem.at[2, q]))
        far[-1].start()
    for q in range(PIECES):
        part = pl.ds(q * step, step)
        near[1, q].wait_recv()
        own = partial[part, columns(me, width)] + near_in[1, part]
        far[q].wait_recv()
        out[part] = first[part, columns(me, width)] - (own + far_in[part])
    for copy in list(near.values()) + far:
        copy.wait_send()


def ring_kernel(n, streams, work, out, slots, send_sem, recv_sem):
    me = lax.axis_index("rows")
    odd = lax.rem(me, 2)
    place = (1 - odd) * lax.div(me, 2) + odd * (n - 1 - lax.div(me, 2))

    def device(position):
        late = lax.div(position, n // 2)
        return (1 - late) * 2 * position + late * (2 * (n - 1 - position) + 1)

    up = device(lax.rem(place + 1, n))
    down = device(lax.rem(place + n - 1, n))
    greet("rows", (up, down))
    cuts = work.shape[1] // slots.shape[2]
    lane_blocks = streams // cuts
    width, tall = work.shape[2] // lane_blocks, slots.shape[2]

    def target(stream):
        return up if stream < streams // 2 else down

    def chunk(stream, step):
        sign = -1 if stream < streams // 2 else 1
        return lax.rem(place + sign * step + 2 * n, n)

    def lanes(stream):
        return pl.ds(stream // cuts * width, width)

    def band(stream):
        return pl.ds(stream % cuts * tall, tall)

    def reducing(stream, step, source):
        return send("rows", target(stream), source, slots.at[stream, step], send_sem.at[0, stream, step], recv_sem.at[0, stream, step])

    def sharing(stream, step):
        held = out.at[chunk(stream, step - 1), band(stream), lanes(stream)]
        return send("rows", target(stream), held, held, send_sem.at[1, stream, step], recv_sem.at[1, stream, step])

    for stream in range(streams):
        reducing(stream, 0, work.at[chunk(stream, 0), band(stream), lanes(stream)]).start()

    def reduce_step(step, carry):
        for stream in range(streams):
            slot = slots.at[stream, step - 1]
            reducing(stream, step - 1, slot).wait_recv()
            slot[...] = slot[...] + work[chunk(stream, step), band(stream), lanes(stream)]
            reducing(stream, step, slot).start()
        return carry

    lax.fori_loop(1, n - 1, reduce_step, 0)
    for stream in range(streams):
        reducing(stream, n - 2, slots.at[stream, n - 2]).wait_recv()
        own = chunk(stream, n - 1)
        out[own, band(stream), lanes(stream)] = slots[stream, n - 2] + work[own, band(stream), lanes(stream)]
        sharing(stream, 0).start()

    def share_step(step, carry):
        for stream in range(streams):
            sharing(stream, step - 1).wait_recv()
            sharing(stream, step).start()
        return carry

    lax.fori_loop(1, n - 1, share_step, 0)
    for stream in range(streams):
        sharing(stream, n - 2).wait_recv()

    def drain(step, carry):
        for stream in range(streams):
            reducing(stream, step, slots.at[stream, step]).wait_send()
            sharing(stream, step).wait_send()
        return carry

    lax.fori_loop(0, n - 1, drain, 0)


def gram_kernel(n, work, out, held, send_sem, recv_sem):
    me = lax.axis_index("rows")
    peers = [lax.rem(me + d, n) for d in range(1, n)]
    greet("rows", peers)
    parts, wholes = [], []
    for d, peer in enumerate(peers):
        parts.append(send("rows", peer, work.at[peer], held.at[d], send_sem.at[0, d], recv_sem.at[0, d]))
        parts[-1].start()
    total = work[me]
    for d in range(n - 1):
        parts[d].wait_recv()
        total = total + held[d]
    out[me] = total
    for d, peer in enumerate(peers):
        wholes.append(send("rows", peer, out.at[me], out.at[me], send_sem.at[1, d], recv_sem.at[1, d]))
        wholes[-1].start()
    for copy in wholes:
        copy.wait_recv()
    for copy in parts + wholes:
        copy.wait_send()


def factor_kernel(gram, factor, solved):
    size, tile = gram.shape[1], 8
    lane = lax.broadcasted_iota(jnp.int32, (1, size), 1)
    below = lax.broadcasted_iota(jnp.int32, (tile, size), 0)
    for b in range(gram.shape[0]):
        left = [gram[b, pl.ds(i * tile, tile), :] for i in range(size // tile)]
        right = [
            jnp.where(lax.broadcasted_iota(jnp.int32, (tile, size), 1) == below + i * tile, 1.0, 0.0)
            for i in range(size // tile)
        ]
        for j in range(size):
            at, r = j // tile, j % tile
            row = left[at][r : r + 1, :]
            scale = 1.0 / jnp.sqrt(jnp.broadcast_to(row[:, j : j + 1], (1, size)))
            upper = jnp.where(lane >= j, row * scale, 0.0)
            inner = right[at][r : r + 1, :] * scale
            factor[b, j : j + 1, :] = upper
            solved[b, j : j + 1, :] = inner
            upper, inner = upper * scale, inner * scale
            for i in range(at, size // tile):
                column = jnp.broadcast_to(left[i][:, j : j + 1], (tile, size))
                if i == at:
                    column = jnp.where(below > r, column, 0.0)
                left[i] = left[i] - column * upper
                right[i] = right[i] - column * inner


def call(kernel, key, shape, scratch, counts, *arrays):
    return pl.pallas_call(
        kernel,
        out_shape=jax.ShapeDtypeStruct(shape, F32),
        in_specs=[pl.BlockSpec(memory_space=pltpu.VMEM)] * len(arrays),
        out_specs=pl.BlockSpec(memory_space=pltpu.VMEM),
        scratch_shapes=[pltpu.VMEM(s, F32) for s in scratch]
        + [pltpu.SemaphoreType.DMA(counts), pltpu.SemaphoreType.DMA(counts)],
        compiler_params=pltpu.CompilerParams(
            collective_id=key, has_side_effects=True, vmem_limit_bytes=48 * 1024 * 1024
        ),
    )(*arrays)


def sum_rows(x, key):
    n = lax.axis_size("rows")
    deep = x.reshape(n, x.shape[0] // n, x.shape[1])
    cuts = 2 if deep.shape[1] >= 32 else 1
    streams = x.shape[1] // BLK * cuts
    total = call(
        functools.partial(ring_kernel, n, streams),
        key,
        deep.shape,
        [(streams, n - 1, deep.shape[1] // cuts, BLK)],
        (2, streams, n - 1),
        deep,
    )
    return total.reshape(x.shape)


def body(basis, block):
    highest, high = lax.Precision.HIGHEST, lax.Precision.HIGH
    rows, width = block.shape
    n = lax.axis_size("rows")
    wide = width * lax.axis_size("cols")
    inverse = 1.0 / (rows * n)

    def project(piece):
        return (
            lax.dot_general(
                basis, piece, (((0,), (0,)), ((), ())), precision=high, preferred_element_type=F32
            )
            * inverse
        )

    def expand(coef):
        return jnp.dot(basis, coef, precision=high, preferred_element_type=F32)

    piece = (PIECES, rows // 2 // PIECES, wide)
    gathered = call(gather_kernel, 0, (rows, wide), [], (3, PIECES), block)
    coef_one = sum_rows(project(gathered), 1)
    first = call(first_kernel, 2, (rows, wide), [piece] * 3, (3, PIECES), expand(coef_one), gathered)
    coef_two = sum_rows(project(first), 3)
    second = call(
        second_kernel,
        4,
        (rows, width),
        [(2, rows, width), (rows, width), (rows, width)],
        (3, PIECES),
        expand(coef_two),
        first,
    )
    blocks = width // BLK
    pieces = second.reshape(rows, blocks, BLK)
    gram = jnp.einsum("mbi,mbj->bij", pieces, pieces, precision=highest) * inverse
    deep = gram.reshape(n, blocks * BLK // n, BLK)
    gram = call(functools.partial(gram_kernel, n), 5, deep.shape, [(n - 1,) + deep.shape[1:]], (2, n - 1), deep)
    gram = gram.reshape(blocks, BLK, BLK)
    factors, solved = pl.pallas_call(
        factor_kernel,
        out_shape=[jax.ShapeDtypeStruct(gram.shape, F32)] * 2,
        in_specs=[pl.BlockSpec(memory_space=pltpu.VMEM)],
        out_specs=[pl.BlockSpec(memory_space=pltpu.VMEM)] * 2,
    )(gram)
    ortho = jnp.einsum("mbi,bji->mbj", pieces, solved, precision=highest).reshape(rows, width)
    return (ortho, factors)


def solution(mesh):
    placed = (P("rows", "cols"), P("rows", "cols"))
    return jax.shard_map(
        body,
        mesh=mesh,
        in_specs=placed,
        out_specs=(P("rows", "cols"), P("cols", None, None)),
        check_vma=False,
    )
```

time: 476 us -> 222 us (0.47)
  waiting for transfers between devices: 383 us -> 0 us
  Pallas kernels: 0 us -> 193 us
  matrix products: 50.5 us -> 20.3 us
  other arithmetic: 23.7 us -> 0 us
  between operations: 14.2 us -> 0.77 us
    psum x4 -> x0, waiting for transfers between devices: 325 us -> none  [the longest x1 102 us: body(): coef_two = lax.psum(terms_two, 'rows')]
    pallas_call x0 -> x7, Pallas kernels: none -> 193 us  [the longest x6 179 us: call(): pl.pallas_call(kernel, out_shape=jax.ShapeDtypeStruct(shape, F32), in_spe...]
    reduce_scatter x1 -> x0, waiting for transfers between devices: 30.3 us -> none  [body(): lax.psum_scatter(expand(coef_two), 'cols', scatter_dimension=1, tiled=True)]
    dot_general x4 -> x5, matrix products: 47.4 us -> 19.3 us  [the longest x2 11 us: project(): lax.dot_general(basis, piece, (((0,), (0,)), ((), ())), precision=high, p...]
    all_gather x1 -> x0, waiting for transfers between devices: 27.2 us -> none  [body(): terms_one = project(lax.all_gather(block, 'cols', axis=1, tiled=True))]
    another operation x4 -> x0, other arithmetic: 22.2 us -> none  [the longest x3 12.4 us: body(): lower_factor = jnp.linalg.cholesky(gram)]
  transfers between devices with their start and end apart: 6 -> 0, of which waited for: 6 -> 0; matrix products, arithmetic and copies ran while one was open for 0% -> 0% of each run, Pallas kernels for 0% -> 0%
where the time goes in v1:
time: 222 us; the launch traced here: 221 us
  Pallas kernels  193 us (87%)
  matrix products  20.3 us (9%)
  local copies, waits for them, and re-layouts  7.16 us (3%)
    pallas_call x6, Pallas kernels, call(): pl.pallas_call(kernel, out_shape=jax.ShapeDtypeStruct(shape, F32), in_spe...  179 us
    pallas_call x1, Pallas kernels, body(): pl.pallas_call(factor_kernel, out_shape=[jax.ShapeDtypeStruct(gram.shape,...  14.3 us
    dot_general x2, matrix products, project(): lax.dot_general(basis, piece, (((0,), (0,)), ((), ())), precision=high, p...  11 us
    dot_general x2, matrix products, expand(): return jnp.dot(basis, coef, precision=high, preferred_element_type=F32)  6.86 us

profile of v1, /device:TPU:0, one launch (start us, length us, event | category | flops | bytes accessed | tf_op | source)
XLA Modules:
  0.0 221.2 jit_solution(5545319933848599554)
XLA Ops:
  0.6 0.0 copy-start.2
  0.6 1.0 copy-done.2
  1.7 16.8 %shard_map.41.base = f32[1024,512]{1,0:T(8,128)S(1)} custom-call(f32[1024,128]{1,0:T(8,128)S(1)} %copy-done.2), custom_call_target="tpu_custom_call" | custom-call | tf_op jit(solution)/shard_map/pallas_call | solution.py:256
  18.5 0.0 copy-start
  18.5 6.1 %convolution_multiply_fusion = f32[1024,512]{1,0:T(8,128)S(1)} fusion(f32[1024,1024]{1,0:T(8,128)} %param.2, f32[1024,512]{1,0:T(8,128)S(1)} %shard_map.41.base), kind=kOutput, calls=%fused_computation.3 | convolution fusion | flops 3221749760 | bytes 8388608 | tf_op jit(solution)/shard_map/dot_general | solution.py:294
  24.5 0.0 copy-done
  24.6 0.0 copy-start.4
  24.6 54.0 %shard_map.42 = f32[8,128,512]{2,1,0:T(8,128)S(1)} custom-call(f32[8,128,512]{2,1,0:T(8,128)S(1)} %bitcast.35), custom_call_target="tpu_custom_call" | custom-call | tf_op jit(solution)/shard_map/pallas_call | solution.py:256
  78.6 0.0 copy-done.4
  78.6 3.4 %convolution_bitcast_fusion.1.partial = f32[1024,512]{1,0:T(8,128)S(1)} fusion(f32[1024,512]{1,0:T(8,128)S(1)} %bitcast.33, f32[1024,1024]{1,0:T(8,128)S(1)} %copy-done.4), kind=kOutput, calls=%fused_computation.2 | convolution fusion | flops 3221225472 | bytes 8388608 | tf_op jit(solution)/shard_map/dot_general | solution.py:301
  82.0 29.5 %shard_map.43.first = f32[1024,512]{1,0:T(8,128)S(1)} custom-call(f32[1024,512]{1,0:T(8,128)S(1)} %convolution_bitcast_fusion.1.partial, f32[1024,512]{1,0:T(8,128)} %copy-done), custom_call_target="tpu_custom_call" | custom-call | tf_op jit(solution)/shard_map/pallas_call | solution.py:256
  111.5 4.9 %multiply_bitcast_fusion = f32[1024,512]{0,1:T(8,128)} fusion(f32[1024,512]{1,0:T(8,128)S(1)} %shard_map.43.first, f32[1024,1024]{1,0:T(8,128)S(1)} %copy-done.4), kind=kOutput, calls=%fused_computation | convolution fusion | flops 3221749760 | bytes 8388608 | tf_op jit(solution)/shard_map/dot_general | solution.py:294
  116.4 2.9 %copy.5 = f32[1024,512]{1,0:T(8,128)} copy(f32[1024,512]{0,1:T(8,128)} %multiply_bitcast_fusion) | data formatting | bytes 4194304 | tf_op jit(solution)/shard_map/mul | solution.py:294
  119.3 0.0 copy-start.1
  119.3 1.6 copy-done.1
  120.9 0.0 copy-start.5
  120.9 52.7 %shard_map.44 = f32[8,128,512]{2,1,0:T(8,128)S(1)} custom-call(f32[8,128,512]{2,1,0:T(8,128)S(1)} %bitcast.32), custom_call_target="tpu_custom_call" | custom-call | tf_op jit(solution)/shard_map/pallas_call | solution.py:256
  173.6 0.0 copy-done.5
  173.6 3.4 %convolution_bitcast_fusion.partial = f32[1024,512]{1,0:T(8,128)S(1)} fusion(f32[1024,512]{1,0:T(8,128)S(1)} %bitcast.34, f32[1024,1024]{1,0:T(8,128)S(1)} %copy-done.5), kind=kOutput, calls=%fused_computation.1 | convolution fusion | flops 3221225472 | bytes 8388608 | tf_op jit(solution)/shard_map/dot_general | solution.py:301
  177.0 15.5 %shard_map.45 = f32[1024,128]{1,0:T(8,128)S(1)} custom-call(f32[1024,512]{1,0:T(8,128)S(1)} %convolution_bitcast_fusion.partial, f32[1024,512]{1,0:T(8,128)S(1)} %shard_map.43.first), custom_call_target="tpu_custom_call" | custom-call | tf_op jit(solution)/shard_map/pallas_call | solution.py:256
  192.6 1.0 convolution_multiply_fusion.1
  193.6 10.2 %shard_map.46 = f32[8,16,128]{2,1,0:T(8,128)S(1)} custom-call(f32[8,16,128]{2,1,0:T(8,128)S(1)} %bitcast.36), custom_call_target="tpu_custom_call" | custom-call | tf_op jit(solution)/shard_map/pallas_call | solution.py:256
  203.8 0.0 copy-start.3
  203.8 0.6 copy-done.3
  204.4 14.3 %shard_map.47 = (f32[1,128,128]{2,1,0:T(8,128)}, f32[1,128,128]{2,1,0:T(8,128)}) custom-call(f32[1,128,128]{2,1,0:T(8,128)} %bitcast.37), custom_call_target="tpu_custom_call" | custom-call | tf_op jit(solution)/shard_map/pallas_call | solution.py:323
  218.7 1.4 convolution_bitcast_fusion.2
  220.2 1.0 copy.7
Async XLA Ops:
  0.6 1.0 copy-start.2
  18.5 6.1 %copy-start = (f32[1024,512]{1,0:T(8,128)}, f32[1024,512]{1,0:T(8,128)S(1)}, u32[]{:S(2)}) copy-start(f32[1024,512]{1,0:T(8,128)S(1)} %shard_map.41.base) | copy-start | bytes 6291460
  24.6 54.0 %copy-start.4 = (f32[1024,1024]{1,0:T(8,128)S(1)}, f32[1024,1024]{1,0:T(8,128)}, u32[]{:S(2)}) copy-start(f32[1024,1024]{1,0:T(8,128)} %param.2) | copy-start | bytes 12582916
  119.3 1.6 copy-start.1
  120.9 52.7 %copy-start.5 = (f32[1024,1024]{1,0:T(8,128)S(1)}, f32[1024,1024]{1,0:T(8,128)}, u32[]{:S(2)}) copy-start(f32[1024,1024]{1,0:T(8,128)} %param.2) | copy-start | bytes 12582916
  203.8 0.6 copy-start.3

commit v2 on v1

--- a/solution.py
+++ b/solution.py
@@ -8,7 +8,7 @@
 from jax.sharding import PartitionSpec as P
 
 BLK = 128
-PIECES = 4
+PIECES = 8
 MESH = pl.DeviceIdType.MESH
 F32 = jnp.float32
 
@@ -69,7 +69,7 @@
         copy.wait_send()
 
 
-def first_kernel(partial, base, out, near_in, chip, far_in, send_sem, recv_sem):
+def first_kernel(partial, base, out, own, near_in, chip, far_in, send_sem, recv_sem):
     me, core, side, mate, across = partners()
     greet("cols", (mate, across))
     half = partial.shape[0] // 2
@@ -93,11 +93,13 @@
     for q in range(PIECES):
         far[q].wait_recv()
         out[mine(q)] = base[mine(q)] - (chip[q] + far_in[q])
+        own[mine(q)] = out[mine(q), columns(me, own.shape[1])]
         held = out.at[mine(q)]
         back.append(send("cols", mate, held, held, send_sem.at[2, q], recv_sem.at[2, q]))
         back[-1].start()
     for q in range(PIECES):
         back[q].wait_recv()
+        own[others(q)] = out[others(q), columns(me, own.shape[1])]
     for copy in near + far + back:
         copy.wait_send()
 
@@ -125,12 +127,12 @@
         near[1, q].wait_recv()
         own = partial[part, columns(me, width)] + near_in[1, part]
         far[q].wait_recv()
-        out[part] = first[part, columns(me, width)] - (own + far_in[part])
+        out[part] = first[part] - (own + far_in[part])
     for copy in list(near.values()) + far:
         copy.wait_send()
 
 
-def ring_kernel(n, streams, work, out, slots, send_sem, recv_sem):
+def ring_kernel(n, work, out, slots, send_sem, recv_sem):
     me = lax.axis_index("rows")
     odd = lax.rem(me, 2)
     place = (1 - odd) * lax.div(me, 2) + odd * (n - 1 - lax.div(me, 2))
@@ -142,65 +144,79 @@
     up = device(lax.rem(place + 1, n))
     down = device(lax.rem(place + n - 1, n))
     greet("rows", (up, down))
-    cuts = work.shape[1] // slots.shape[2]
-    lane_blocks = streams // cuts
-    width, tall = work.shape[2] // lane_blocks, slots.shape[2]
-
-    def target(stream):
-        return up if stream < streams // 2 else down
-
-    def chunk(stream, step):
-        sign = -1 if stream < streams // 2 else 1
-        return lax.rem(place + sign * step + 2 * n, n)
-
-    def lanes(stream):
-        return pl.ds(stream // cuts * width, width)
+    streams, tall = slots.shape[0], slots.shape[2]
+    lane_blocks = streams // 4
+
+    def sign(stream):
+        return 1 - 2 * (stream % 2)
 
     def band(stream):
-        return pl.ds(stream % cuts * tall, tall)
-
-    def reducing(stream, step, source):
-        return send("rows", target(stream), source, slots.at[stream, step], send_sem.at[0, stream, step], recv_sem.at[0, stream, step])
+        return stream // 2 // lane_blocks
+
+    def reach(stream):
+        return n // 2 - (stream % 2 + band(stream)) % 2
+
+    def place_of(stream):
+        return pl.ds(band(stream) * tall, tall), pl.ds(stream // 2 % lane_blocks * BLK, BLK)
+
+    def chunk(offset):
+        return lax.rem(place + offset + 2 * n, n)
+
+    def move(phase, stream, step, source, target):
+        device_id = up if stream % 2 == 0 else down
+        return send("rows", device_id, source, target, send_sem.at[phase, stream, step], recv_sem.at[phase, stream, step])
+
+    def reducing(stream, step, source=None):
+        slot = slots.at[stream, step]
+        return move(0, stream, step, slot if source is None else source, slot)
 
     def sharing(stream, step):
-        held = out.at[chunk(stream, step - 1), band(stream), lanes(stream)]
-        return send("rows", target(stream), held, held, send_sem.at[1, stream, step], recv_sem.at[1, stream, step])
-
-    for stream in range(streams):
-        reducing(stream, 0, work.at[chunk(stream, 0), band(stream), lanes(stream)]).start()
-
-    def reduce_step(step, carry):
-        for stream in range(streams):
-            slot = slots.at[stream, step - 1]
-            reducing(stream, step - 1, slot).wait_recv()
-            slot[...] = slot[...] + work[chunk(stream, step), band(stream), lanes(stream)]
-            reducing(stream, step, slot).start()
-        return carry
-
-    lax.fori_loop(1, n - 1, reduce_step, 0)
-    for stream in range(streams):
-        reducing(stream, n - 2, slots.at[stream, n - 2]).wait_recv()
-        own = chunk(stream, n - 1)
-        out[own, band(stream), lanes(stream)] = slots[stream, n - 2] + work[own, band(stream), lanes(stream)]
-        sharing(stream, 0).start()
-
-    def share_step(step, carry):
-        for stream in range(streams):
-            sharing(stream, step - 1).wait_recv()
-            sharing(stream, step).start()
-        return carry
-
-    lax.fori_loop(1, n - 1, share_step, 0)
-    for stream in range(streams):
-        sharing(stream, n - 2).wait_recv()
-
-    def drain(step, carry):
-        for stream in range(streams):
-            reducing(stream, step, slots.at[stream, step]).wait_send()
-            sharing(stream, step).wait_send()
-        return carry
-
-    lax.fori_loop(0, n - 1, drain, 0)
+        held = out.at[(chunk(-sign(stream) * step), *place_of(stream))]
+        return move(1, stream, step, held, held)
+
+    def reduce_one(stream, step):
+        slot = slots.at[stream, step - 1]
+        reducing(stream, step - 1).wait_recv()
+        slot[...] = slot[...] + work[(chunk(sign(stream) * (reach(stream) - step)), *place_of(stream))]
+        reducing(stream, step, slot).start()
+
+    def share_one(stream, step):
+        sharing(stream, step - 1).wait_recv()
+        sharing(stream, step).start()
+
+    def drain_one(stream, step):
+        reducing(stream, step).wait_send()
+        sharing(stream, step).wait_send()
+
+    every = range(streams)
+    longer = [stream for stream in every if reach(stream) == n // 2]
+
+    def sweep(one, begin):
+        def each(step, carry):
+            for stream in every:
+                one(stream, step)
+            return carry
+
+        lax.fori_loop(begin, n // 2 - 1, each, 0)
+        for stream in longer:
+            one(stream, n // 2 - 1)
+
+    for stream in every:
+        reducing(stream, 0, work.at[(chunk(sign(stream) * reach(stream)), *place_of(stream))]).start()
+    sweep(reduce_one, 1)
+    for pair in range(0, streams, 2):
+        own = (chunk(0), *place_of(pair))
+        total = work[own]
+        for stream in (pair, pair + 1):
+            reducing(stream, reach(stream) - 1).wait_recv()
+            total = total + slots[stream, reach(stream) - 1]
+        out[own] = total
+        for stream in (pair, pair + 1):
+            sharing(stream, 0).start()
+    sweep(share_one, 1)
+    for stream in every:
+        sharing(stream, reach(stream) - 1).wait_recv()
+    sweep(drain_one, 0)
 
 
 def gram_kernel(n, work, out, held, send_sem, recv_sem):
@@ -255,13 +271,15 @@
 def call(kernel, key, shape, scratch, counts, *arrays):
     return pl.pallas_call(
         kernel,
-        out_shape=jax.ShapeDtypeStruct(shape, F32),
+        out_shape=jax.tree.map(lambda s: jax.ShapeDtypeStruct(s, F32), shape, is_leaf=lambda s: isinstance(s[0], int)),
         in_specs=[pl.BlockSpec(memory_space=pltpu.VMEM)] * len(arrays),
-        out_specs=pl.BlockSpec(memory_space=pltpu.VMEM),
+        out_specs=jax.tree.map(
+            lambda s: pl.BlockSpec(memory_space=pltpu.VMEM), shape, is_leaf=lambda s: isinstance(s[0], int)
+        ),
         scratch_shapes=[pltpu.VMEM(s, F32) for s in scratch]
         + [pltpu.SemaphoreType.DMA(counts), pltpu.SemaphoreType.DMA(counts)],
         compiler_params=pltpu.CompilerParams(
-            collective_id=key, has_side_effects=True, vmem_limit_bytes=48 * 1024 * 1024
+            collective_id=key, has_side_effects=True, vmem_limit_bytes=16 * 1024 * 1024
         ),
     )(*arrays)
 
@@ -269,14 +287,13 @@
 def sum_rows(x, key):
     n = lax.axis_size("rows")
     deep = x.reshape(n, x.shape[0] // n, x.shape[1])
-    cuts = 2 if deep.shape[1] >= 32 else 1
-    streams = x.shape[1] // BLK * cuts
+    streams = 4 * (x.shape[1] // BLK)
     total = call(
-        functools.partial(ring_kernel, n, streams),
+        functools.partial(ring_kernel, n),
         key,
         deep.shape,
-        [(streams, n - 1, deep.shape[1] // cuts, BLK)],
-        (2, streams, n - 1),
+        [(streams, n // 2, deep.shape[1] // 2, BLK)],
+        (2, streams, n // 2),
         deep,
     )
     return total.reshape(x.shape)
@@ -303,7 +320,7 @@
     piece = (PIECES, rows // 2 // PIECES, wide)
     gathered = call(gather_kernel, 0, (rows, wide), [], (3, PIECES), block)
     coef_one = sum_rows(project(gathered), 1)
-    first = call(first_kernel, 2, (rows, wide), [piece] * 3, (3, PIECES), expand(coef_one), gathered)
+    first, own = call(first_kernel, 2, [(rows, wide), (rows, width)], [piece] * 3, (3, PIECES), expand(coef_one), gathered)
     coef_two = sum_rows(project(first), 3)
     second = call(
         second_kernel,
@@ -312,7 +329,7 @@
         [(2, rows, width), (rows, width), (rows, width)],
         (3, PIECES),
         expand(coef_two),
-        first,
+        own,
     )
     blocks = width // BLK
     pieces = second.reshape(rows, blocks, BLK)

time: 222 us -> 205 us (0.923)
  Pallas kernels: 193 us -> 179 us
  local copies, waits for them, and re-layouts: 7.16 us -> 4.59 us
    pallas_call x6, Pallas kernels: 179 us -> 165 us  [call(): pl.pallas_call(kernel, out_shape=jax.tree.map(lambda s: jax.ShapeDtypeStr...]
where the time goes in v2:
time: 205 us
  Pallas kernels  179 us (87%)
  matrix products  20.1 us (10%)
  local copies, waits for them, and re-layouts  4.59 us (2%)
    pallas_call x6, Pallas kernels, call(): pl.pallas_call(kernel, out_shape=jax.tree.map(lambda s: jax.ShapeDtypeStr...  165 us
    pallas_call x1, Pallas kernels, body(): pl.pallas_call(factor_kernel, out_shape=[jax.ShapeDtypeStruct(gram.shape,...  14.3 us
    dot_general x2, matrix products, project(): lax.dot_general(basis, piece, (((0,), (0,)), ((), ())), precision=high, p...  10.6 us
    dot_general x2, matrix products, expand(): return jnp.dot(basis, coef, precision=high, preferred_element_type=F32)  7.07 us

profile of v2, /device:TPU:0, one launch (start us, length us, event | category | flops | bytes accessed | tf_op | source)
XLA Modules:
  0.0 204.8 jit_solution(2138685880812155227)
XLA Ops:
  0.6 0.0 copy-start
  0.6 1.0 copy-done
  1.7 16.9 %shard_map.41.base = f32[1024,512]{1,0:T(8,128)S(1)} custom-call(f32[1024,128]{1,0:T(8,128)S(1)} %copy-done), custom_call_target="tpu_custom_call" | custom-call | tf_op jit(solution)/shard_map/pallas_call | solution.py:272
  18.6 5.5 %convolution_multiply_fusion = f32[1024,512]{1,0:T(8,128)S(1)} fusion(f32[1024,1024]{1,0:T(8,128)} %param.2, f32[1024,512]{1,0:T(8,128)S(1)} %shard_map.41.base), kind=kOutput, calls=%fused_computation.3 | convolution fusion | flops 3221749760 | bytes 8388608 | tf_op jit(solution)/shard_map/dot_general | solution.py:311
  24.1 0.0 copy-start.2
  24.1 47.8 %shard_map.42 = f32[8,128,512]{2,1,0:T(8,128)S(1)} custom-call(f32[8,128,512]{2,1,0:T(8,128)S(1)} %bitcast.35), custom_call_target="tpu_custom_call" | custom-call | tf_op jit(solution)/shard_map/pallas_call | solution.py:272
  71.9 0.0 copy-done.2
  71.9 3.5 %convolution_bitcast_fusion.1.partial = f32[1024,512]{1,0:T(8,128)S(1)} fusion(f32[1024,512]{1,0:T(8,128)S(1)} %bitcast.33, f32[1024,1024]{1,0:T(8,128)S(1)} %copy-done.2), kind=kOutput, calls=%fused_computation.2 | convolution fusion | flops 3221225472 | bytes 8388608 | tf_op jit(solution)/shard_map/dot_general | solution.py:318
  75.5 27.7 %shard_map.43 = (f32[1024,512]{1,0:T(8,128)S(1)}, f32[1024,128]{1,0:T(8,128)S(1)}) custom-call(f32[1024,512]{1,0:T(8,128)S(1)} %convolution_bitcast_fusion.1.partial, f32[1024,512]{1,0:T(8,128)S(1)} %shard_map.41.base), custom_call_target="tpu_custom_call" | custom-call | tf_op jit(solution)/shard_map/pallas_call | solution.py:272
  103.1 5.1 %multiply_bitcast_fusion = f32[1024,512]{0,1:T(8,128)} fusion(f32[1024,512]{1,0:T(8,128)S(1)} %get-tuple-element.6, f32[1024,1024]{1,0:T(8,128)S(1)} %copy-done.2), kind=kOutput, calls=%fused_computation | convolution fusion | flops 3221749760 | bytes 8388608 | tf_op jit(solution)/shard_map/dot_general | solution.py:311
  108.3 1.9 copy.5
  110.2 0.0 copy-start.3
  110.2 46.1 %shard_map.44 = f32[8,128,512]{2,1,0:T(8,128)S(1)} custom-call(f32[8,128,512]{2,1,0:T(8,128)S(1)} %bitcast.32), custom_call_target="tpu_custom_call" | custom-call | tf_op jit(solution)/shard_map/pallas_call | solution.py:272
  156.3 0.0 copy-done.3
  156.3 3.5 %convolution_bitcast_fusion.partial = f32[1024,512]{1,0:T(8,128)S(1)} fusion(f32[1024,512]{1,0:T(8,128)S(1)} %bitcast.34, f32[1024,1024]{1,0:T(8,128)S(1)} %copy-done.3), kind=kOutput, calls=%fused_computation.1 | convolution fusion | flops 3221225472 | bytes 8388608 | tf_op jit(solution)/shard_map/dot_general | solution.py:318
  159.9 15.3 %shard_map.45 = f32[1024,128]{1,0:T(8,128)S(1)} custom-call(f32[1024,512]{1,0:T(8,128)S(1)} %convolution_bitcast_fusion.partial, f32[1024,128]{1,0:T(8,128)S(1)} %get-tuple-element.7.first), custom_call_target="tpu_custom_call" | custom-call | tf_op jit(solution)/shard_map/pallas_call | solution.py:272
  175.2 1.0 convolution_multiply_fusion.1
  176.3 11.1 %shard_map.46 = f32[8,16,128]{2,1,0:T(8,128)S(1)} custom-call(f32[8,16,128]{2,1,0:T(8,128)S(1)} %bitcast.36), custom_call_target="tpu_custom_call" | custom-call | tf_op jit(solution)/shard_map/pallas_call | solution.py:272
  187.4 0.0 copy-start.1
  187.4 0.6 copy-done.1
  188.0 14.3 %shard_map.47 = (f32[1,128,128]{2,1,0:T(8,128)}, f32[1,128,128]{2,1,0:T(8,128)}) custom-call(f32[1,128,128]{2,1,0:T(8,128)} %bitcast.37), custom_call_target="tpu_custom_call" | custom-call | tf_op jit(solution)/shard_map/pallas_call | solution.py:340
  202.4 1.4 convolution_bitcast_fusion.2
  203.8 1.0 copy.7
Async XLA Ops:
  0.6 1.0 copy-start
  24.1 47.8 %copy-start.2 = (f32[1024,1024]{1,0:T(8,128)S(1)}, f32[1024,1024]{1,0:T(8,128)}, u32[]{:S(2)}) copy-start(f32[1024,1024]{1,0:T(8,128)} %param.2) | copy-start | bytes 12582916
  110.2 46.1 %copy-start.3 = (f32[1024,1024]{1,0:T(8,128)S(1)}, f32[1024,1024]{1,0:T(8,128)}, u32[]{:S(2)}) copy-start(f32[1024,1024]{1,0:T(8,128)} %param.2) | copy-start | bytes 12582916
  187.4 0.6 copy-start.1
